TPU v7x, 128 devices: a whole 4x4x4 slice. The times are simulated.
128 devices in a mesh: row: 16 (over z_hi, x, core), col: 8 (over y, z_lo).
Axes of the slice: x: 4, y: 4, z: 4 (z_hi: 2, z_lo: 2; z = z_hi * 2 + z_lo), core: 2. Of those that a mesh axis runs over, the one named last changes fastest.
Arguments:
- pair: bfloat16 [512, 512, 128], P('row', 'col'), may hold values from -6 to 6
- cotangent: bfloat16 [512, 512, 128], P('row', 'col'), may hold values from -6 to 6
- length: int32 [1], replicated, may hold values from 256 to 512
- norm_gain: float32 [128], replicated, may hold values from 0.1 to 1.9
- norm_bias: float32 [128], replicated, may hold values from -1.5 to 1.5
- left_weight: bfloat16 [128, 256], replicated, may hold values from -0.5 to 0.5
- right_weight: bfloat16 [128, 256], replicated, may hold values from -0.5 to 0.5
- gate_weight: bfloat16 [128, 128], replicated, may hold values from -0.5 to 0.5
- out_gain: float32 [128], replicated, may hold values from 0.1 to 1.9
- out_bias: float32 [128], replicated, may hold values from -2 to 2
- out_weight: bfloat16 [128, 128], replicated, may hold values from -0.5 to 0.5
Outputs:
- update: bfloat16 [512, 512, 128], P('row', 'col')
- grad_pair: bfloat16 [512, 512, 128], P('row', 'col')
- grad_left: float32 [128, 256], replicated
- grad_right: float32 [128, 256], replicated
- grad_gating: float32 [128, 128], replicated
- grad_output: float32 [128, 128], replicated
- grad_norms: float32 [4, 128], replicated
Inputs may be any that keep to these rules, and one draw needn't show every extreme that they name: Tokens at positions 511 down to length are padding.
All inputs are finite; a program needn't handle non-finite values.
Results may differ from a plain program's by a relative error of at most 0.014.
Values may be sent and summed in bfloat16 or wider, within the bound.
A program may use at most 128 MiB of HBM per device.

v0:
```python
import jax
import jax.numpy as jnp
from jax import lax
from jax.sharding import PartitionSpec as P

EPS = 1e-05


def broadcast(block, axis, holder):
    block = jnp.where(lax.axis_index(axis) == holder, block, jnp.zeros_like(block))
    return lax.psum(block, axis)


def split_up(x, dim, peers):
    dims = x.shape
    tiles = x.reshape(*dims[:dim], peers, dims[dim] // peers, *dims[dim + 1 :])
    return jnp.moveaxis(tiles, dim, 0)


def summed_on_arrival(x, axis, dim):
    peers = lax.axis_size(axis)
    tiles = lax.all_to_all(split_up(x, dim, peers), axis, 0, 0, tiled=True)
    return jnp.sum(tiles.astype(jnp.float32), axis=0)


def together(arrays, axis):
    flat, at, done = (jnp.concatenate([a.reshape(-1) for a in arrays]), 0, [])
    total = lax.psum(flat, axis)
    for a in arrays:
        done.append(total[at : at + a.size].reshape(a.shape))
        at += a.size
    return tuple(done)


def normalize(values):
    center = values - jnp.mean(values, axis=-1, keepdims=True)
    inverse = lax.rsqrt(jnp.mean(center * center, axis=-1, keepdims=True) + EPS)
    return (center * inverse, inverse)


def gating(panel, weight, first_ok, second_ok, hidden):
    projected = jnp.einsum("ikc,ch->ikh", panel, weight, preferred_element_type=jnp.float32)
    values = projected[..., :hidden]
    sigmoid_val = jax.nn.sigmoid(projected[..., hidden:])
    pad_mask = (first_ok[:, None] & second_ok[None, :]).astype(jnp.float32)[..., None]
    return ((pad_mask * sigmoid_val * values).astype(jnp.bfloat16), values, sigmoid_val, pad_mask)


def push_back(partial_value, values, sigmoid_val, pad_mask, weight, panel):
    combined = jnp.concatenate(
        [
            partial_value * pad_mask * sigmoid_val,
            partial_value * pad_mask * values * sigmoid_val * (1.0 - sigmoid_val),
        ],
        axis=-1,
    ).astype(jnp.bfloat16)
    panel_grad = jnp.einsum("ikh,ch->ikc", combined, weight, preferred_element_type=jnp.float32)
    weight_grad = jnp.einsum("ikc,ikh->ch", panel, combined, preferred_element_type=jnp.float32)
    return (panel_grad, weight_grad)


def per_device(
    pair,
    cotangent,
    length,
    norm_gain,
    norm_bias,
    left_weight,
    right_weight,
    gate_weight,
    out_gain,
    out_bias,
    out_weight,
):
    row_index = lax.axis_index("row")
    col_index = lax.axis_index("col")
    n_row = lax.axis_size("row")
    n_col = lax.axis_size("col")
    per_col = n_row // n_col
    rows_dev = pair.shape[0]
    cols_dev = pair.shape[1]
    tokens = rows_dev * n_row
    hidden = out_weight.shape[0]
    pair_hat, pair_scale = normalize(pair.astype(jnp.float32))
    normed = (pair_hat * norm_gain + norm_bias).astype(jnp.bfloat16)
    real_count = length[0]
    second_ok = jnp.arange(tokens, dtype=jnp.int32) < real_count
    own_ok = row_index * rows_dev + jnp.arange(rows_dev, dtype=jnp.int32) < real_count
    partner_ok = col_index * cols_dev + jnp.arange(cols_dev, dtype=jnp.int32) < real_count
    left_tile, left_val, left_sig, tile_mask = gating(
        normed, left_weight, own_ok, partner_ok, hidden
    )
    right_tile, right_val, right_sig, unused_mask = gating(
        normed, right_weight, own_ok, partner_ok, hidden
    )
    row_panel = lax.all_gather(normed, "col", axis=1, tiled=True)
    pieces = []
    for member in range(per_col):
        pieces.append(broadcast(row_panel, "row", col_index * per_col + member))
    col_panel = jnp.concatenate(pieces, axis=0)
    left_act = gating(row_panel, left_weight, own_ok, second_ok, hidden)[0]
    right_act = gating(col_panel, right_weight, partner_ok, second_ok, hidden)[0]
    tri = jnp.einsum("ikh,jkh->ijh", left_act, right_act, preferred_element_type=jnp.float32)
    tri_hat, tri_scale = normalize(tri)
    tri_normed = (tri_hat * out_gain + out_bias).astype(jnp.bfloat16)
    outer_val = jnp.einsum(
        "ijh,hc->ijc", tri_normed, out_weight, preferred_element_type=jnp.float32
    )
    gate_val = jax.nn.sigmoid(
        jnp.einsum("ijc,cd->ijd", normed, gate_weight, preferred_element_type=jnp.float32)
    )
    update = (gate_val * outer_val).astype(jnp.bfloat16)
    upstream = cotangent.astype(jnp.float32)
    outer_grad = (upstream * gate_val).astype(jnp.bfloat16)
    gate_grad = (upstream * outer_val * gate_val * (1.0 - gate_val)).astype(jnp.bfloat16)
    grad_output = jnp.einsum(
        "ijh,ijc->hc", tri_normed, outer_grad, preferred_element_type=jnp.float32
    )
    grad_gating = jnp.einsum("ijc,ijd->cd", normed, gate_grad, preferred_element_type=jnp.float32)
    tnorm_grad = jnp.einsum(
        "ijc,hc->ijh", outer_grad, out_weight, preferred_element_type=jnp.float32
    )
    hat_grad = tnorm_grad * out_gain
    tri_grad = (
        tri_scale
        * (
            hat_grad
            - jnp.mean(hat_grad, axis=-1, keepdims=True)
            - tri_hat * jnp.mean(hat_grad * tri_hat, axis=-1, keepdims=True)
        )
    ).astype(jnp.bfloat16)
    row_partial = jnp.einsum(
        "ijh,jkh->ikh", tri_grad, right_act, preferred_element_type=jnp.float32
    )
    col_partial = jnp.einsum("ijh,ikh->jkh", tri_grad, left_act, preferred_element_type=jnp.float32)
    row_part = summed_on_arrival(row_partial.astype(jnp.bfloat16), "col", 1)
    summed = lax.psum_scatter(
        col_partial.astype(jnp.bfloat16), "row", scatter_dimension=0, tiled=True
    )
    slab = summed[None]
    received = lax.all_to_all(slab, "col", split_axis=2, concat_axis=0, tiled=True)
    select = (jnp.arange(per_col, dtype=jnp.int32) == row_index // n_col).astype(jnp.bfloat16)
    spread = (received[:, None] * select[None, :, None, None, None]).reshape(
        (n_row,) + received.shape[1:]
    )
    returned = lax.all_to_all(spread, "row", split_axis=0, concat_axis=0, tiled=True)
    start = row_index % per_col * n_col
    owned = lax.dynamic_slice_in_dim(returned, start, n_col, 0).reshape(rows_dev, cols_dev, -1)
    col_part = owned.astype(jnp.float32)
    from_rows, grad_left = push_back(row_part, left_val, left_sig, tile_mask, left_weight, normed)
    from_cols, grad_right = push_back(
        col_part, right_val, right_sig, tile_mask, right_weight, normed
    )
    gate_back = jnp.einsum(
        "ijd,cd->ijc", gate_grad, gate_weight, preferred_element_type=jnp.float32
    )
    normed_grad = gate_back + from_rows + from_cols
    scaled = normed_grad * norm_gain
    grad_pair = (
        pair_scale
        * (
            scaled
            - jnp.mean(scaled, axis=-1, keepdims=True)
            - pair_hat * jnp.mean(scaled * pair_hat, axis=-1, keepdims=True)
        )
    ).astype(jnp.bfloat16)
    grad_norms = jnp.stack(
        [
            jnp.sum(normed_grad * pair_hat, axis=(0, 1)),
            jnp.sum(normed_grad, axis=(0, 1)),
            jnp.sum(tnorm_grad * tri_hat, axis=(0, 1)),
            jnp.sum(tnorm_grad, axis=(0, 1)),
        ]
    )
    totals = together((grad_left, grad_right, grad_gating, grad_output, grad_norms), ("row", "col"))
    inverse = 1.0 / tokens
    return (
        update,
        grad_pair,
        totals[0] * inverse,
        totals[1] * inverse,
        totals[2] * inverse,
        totals[3] * inverse,
        totals[4] * inverse,
    )


def solution(mesh):
    return jax.shard_map(
        per_device,
        mesh=mesh,
        in_specs=(
            P("row", "col", None),
            P("row", "col", None),
            P(),
            P(),
            P(),
            P(),
            P(),
            P(),
            P(),
            P(),
            P(),
        ),
        out_specs=(P("row", "col", None), P("row", "col", None), P(), P(), P(), P(), P()),
        check_vma=False,
    )
```

profile of v0, /device:TPU:1, one launch (start us, length us, event | category | flops | bytes accessed | tf_op | source)
XLA Modules:
  0.0 731.4 jit_solution(15539498948825562416)
XLA Ops:
  7.2 1.4 convert_reduce_fusion.1
  8.6 1.7 fusion.33
  10.3 2.5 fusion.27
  12.9 92.9 %all-gather.2.cloned.1.call-done = bf16[32,512,128]{2,1,0:T(8,128)(2,1)} async-done(((bf16[32,64,128]{2,1,0:T(8,128)(2,1)}), bf16[32,512,128]{2,1,0:T(8,128)(2,1)}) %all-gather.2.cloned.1.call-update) | async-done | bytes 4194320 | tf_op jit(solution)/shard_map/all_gather | solution.py:96
  105.7 5.9 broadcast_select_fusion.1
  112.5 0.2 copy-done.5
  112.7 0.4 fusion.19
  113.2 1.4 fusion.78
  114.6 3.1 copy.55
  117.7 0.1 and_convert_fusion.1
  117.7 0.1 and_convert_fusion
  117.8 4.5 fusion.57
  122.3 4.4 fusion.5
  126.7 8.0 %copy.53 = bf16[32,512,128]{1,0,2:T(8,128)(2,1)} copy(bf16[32,512,128]{2,1,0:T(8,128)(2,1)} %fusion.5) | data formatting | bytes 8388608 | tf_op jit(solution)/shard_map/convert_element_type | solution.py:46
  134.7 140.6 %all-reduce.6.cloned.1.call-done = (bf16[32,512,128]{2,1,0:T(8,128)(2,1)}, bf16[32,512,128]{2,1,0:T(8,128)(2,1)}) async-done(((bf16[32,512,128]{2,1,0:T(8,128)(2,1)}, bf16[32,512,128]{2,1,0:T(8,128)(2,1)}), (bf16[32,512,128]{2,1,0:T(8,128)(2,1)}, bf16[32,512,128]{2,1,0:T(8,128)(2,1)})) %all-reduce.6.cloned.1.call-update) | async-done | bytes 8388624 | tf_op jit(solution)/shard_map/psum | solution.py:11
  275.3 19.0 %fusion.10 = f32[64,512,256]{2,1,0:T(8,128)} fusion(bf16[32,512,128]{2,1,0:T(8,128)(2,1)} %get-tuple-element.14, bf16[32,512,128]{2,1,0:T(8,128)(2,1)} %get-tuple-element.15, bf16[128,256]{1,0:T(8,128)(2,1)S(1)} %copy-done), kind=kOutput, calls=%fused_computation.14 | convolution fusion | flops 2151677952 | bytes 42008576 | tf_op jit(solution)/shard_map/ikc,ch->ikh/dot_general | solution.py:42
  294.3 16.2 %fusion = bf16[64,512,128]{2,1,0:T(8,128)(2,1)} fusion(f32[64,512,256]{2,1,0:T(8,128)} %fusion.10, f32[64,512]{1,0:T(8,128)S(1)} %and_convert_fusion), kind=kLoop, calls=%fused_computation.1 | loop fusion | flops 25165824 | bytes 42074112 | tf_op jit(solution)/shard_map/convert_element_type | solution.py:46
  310.6 12.5 %copy.52 = bf16[64,512,128]{1,0,2:T(8,128)(2,1)} copy(bf16[64,512,128]{2,1,0:T(8,128)(2,1)} %fusion) | data formatting | bytes 16777216 | tf_op jit(solution)/shard_map/convert_element_type | solution.py:46
  323.1 6.9 bitcast_reduce_fusion
  330.0 0.3 multiply_reduce_fusion.2
  330.4 1.3 multiply_reduce_fusion
  331.7 1.9 multiply_convert_fusion
  333.5 1.0 copy-done.2
  334.5 5.6 convert_bitcast_fusion
  340.1 13.0 %copy.60 = bf16[64,512,128]{2,1,0:T(8,128)(2,1)} copy(bf16[64,512,128]{1,0,2:T(8,128)(2,1)} %convert_bitcast_fusion) | data formatting | bytes 16777216 | tf_op jit(solution)/shard_map/convert_element_type | solution.py:138
  353.1 102.8 %reduce-scatter.2.cloned.1.call-done = bf16[4,512,128]{2,1,0:T(8,128)(2,1)} async-done(((bf16[64,512,128]{2,1,0:T(8,128)(2,1)}), bf16[4,512,128]{2,1,0:T(8,128)(2,1)}) %reduce-scatter.2.cloned.1.call-update) | async-done | bytes 524304 | tf_op jit(solution)/shard_map/reduce_scatter | solution.py:137
  455.9 2.2 copy.61
  458.2 4.1 all-to-all-start.1
  462.2 6.6 convert_bitcast_fusion.1
  468.9 7.9 %copy.57 = bf16[32,512,128]{2,1,0:T(8,128)(2,1)} copy(bf16[32,512,128]{1,0,2:T(8,128)(2,1)} %convert_bitcast_fusion.1) | data formatting | bytes 8388608 | tf_op jit(solution)/shard_map/convert_element_type | solution.py:136
  476.7 5.5 copy.58
  482.2 5.3 all-to-all-start
  487.5 0.1 mul.280
  487.6 1.7 fusion.55
  489.4 1.8 fusion.60
  491.2 1.4 bitcast_multiply_fusion
  492.6 53.0 %all-to-all-done = bf16[8,32,64,128]{3,2,1,0:T(8,128)(2,1)} async-done(((bf16[8,32,64,128]{3,2,1,0:T(8,128)(2,1)}), bf16[8,32,64,128]{3,2,1,0:T(8,128)(2,1)}, u32[]{:S(2)}, u32[]{:S(2)}) %all-to-all-start) | async-done | bytes 4194336 | tf_op jit(solution)/shard_map/all_to_all | solution.py:22
  545.6 7.4 %all-to-all-start.2 = ((bf16[16,4,64,128]{3,2,1,0:T(8,128)(2,1)}), bf16[16,4,64,128]{3,2,1,0:T(8,128)(2,1)}, u32[]{:S(2)}, u32[]{:S(2)}) async-start(bf16[16,4,64,128]{3,2,1,0:T(8,128)(2,1)} %bitcast_multiply_fusion), calls=%async_computation.3 | async-start | bytes 2097152 | tf_op jit(solution)/shard_map/all_to_all | solution.py:146
  553.0 0.3 all-reduce.4.cloned.1.call-start
  553.2 0.1 and_convert_fusion.2
  553.3 2.2 copy.54
  555.5 1.2 fusion.36
  556.8 0.8 copy-done.10
  557.5 1.3 fusion.67
  558.8 4.1 convert_reduce_fusion
  563.0 7.4 %all-to-all-done.2 = bf16[16,4,64,128]{3,2,1,0:T(8,128)(2,1)} async-done(((bf16[16,4,64,128]{3,2,1,0:T(8,128)(2,1)}), bf16[16,4,64,128]{3,2,1,0:T(8,128)(2,1)}, u32[]{:S(2)}, u32[]{:S(2)}) %all-to-all-start.2) | async-done | bytes 1048608 | tf_op jit(solution)/shard_map/all_to_all | solution.py:146
  570.3 1.1 constant_dynamic-slice_fusion
  571.4 3.0 fusion.51
  574.5 0.4 convolution_bitcast_fusion.2
  574.9 0.4 convolution_bitcast_fusion.3
  575.4 0.7 constant_dynamic-update-slice_fusion.2
  576.0 0.7 constant_dynamic-update-slice_fusion.1
  576.7 1.0 fusion.15
  577.7 1.0 fusion.14
  578.6 0.4 convolution_add_fusion.1
  579.1 1.2 fusion.32
  580.3 0.6 constant_dynamic-update-slice_fusion
  580.9 2.0 fusion.31
  582.9 136.8 %all-reduce.4.cloned.1.call-done = f32[98816]{0:T(1024)} async-done(((f32[98816]{0:T(1024)}), f32[98816]{0:T(1024)}) %all-reduce.4.cloned.1.call-update) | async-done | bytes 395280 | tf_op jit(solution)/shard_map/psum | solution.py:28
  719.7 1.0 slice_multiply_fusion.4
  720.7 0.7 mul.297
  721.4 0.7 mul.299
  722.1 1.5 fusion.52
  723.6 1.3 fusion.70
  (56 shorter events, 0.6 us)
Async XLA Ops:
  7.2 268.1 %copy-start = (bf16[128,256]{1,0:T(8,128)(2,1)S(1)}, bf16[128,256]{1,0:T(8,128)(2,1)}, u32[]{:S(2)}) copy-start(bf16[128,256]{1,0:T(8,128)(2,1)} %param.17) | copy-start | bytes 196612
  7.2 98.6 %all-gather.2.cloned.1.call-start = ((), (), s32[]{:S(2)}) async-start(), calls=%async_computation.4 | async-start | bytes 4718592 | tf_op jit(solution)/shard_map/all_gather | solution.py:96
  12.8 262.5 %all-reduce.6.cloned.1.call-start = ((), (), s32[]{:S(2)}) async-start(), calls=%async_computation.7 | async-start | bytes 16777216 | tf_op jit(solution)/shard_map/psum | solution.py:11
  111.7 1.0 copy-start.5
  111.7 1.0 copy-start.14
  111.7 1.4 copy-start.7
  111.7 1.4 copy-start.13
  111.7 344.2 %reduce-scatter.2.cloned.1.call-start = ((), (), s32[]{:S(2)}) async-start(), calls=%async_computation.5 | async-start | bytes 8912896 | tf_op jit(solution)/shard_map/reduce_scatter | solution.py:137
  112.7 5.1 copy-start.12
  323.1 7.3 copy-start.16
  330.0 1.7 copy-start.17
  331.6 2.9 copy-start.1
  333.5 1.0 copy-start.2
  353.1 109.2 %copy-start.3 = (bf16[32,64,128]{1,0,2:T(8,128)(2,1)S(1)}, bf16[32,64,128]{1,0,2:T(8,128)(2,1)}, u32[]{:S(2)}) copy-start(bf16[32,64,128]{1,0,2:T(8,128)(2,1)} %copy-done.2) | copy-start | bytes 1572868
  458.2 24.1 %all-to-all-start.1 = ((bf16[1,4,512,128]{3,1,0,2:T(4,128)(2,1)}), bf16[1,4,512,128]{3,1,0,2:T(4,128)(2,1)S(1)}, u32[]{:S(2)}, u32[]{:S(2)}) async-start(bf16[1,4,512,128]{3,1,0,2:T(4,128)(2,1)} %copy.61), calls=%async_computation.2 | async-start | bytes 1048576 | tf_op jit(solution)/shard_map/all_to_all | solution.py:141
  482.2 5.4 copy-start.6
  482.2 63.3 %all-to-all-start = ((bf16[8,32,64,128]{3,2,1,0:T(8,128)(2,1)}), bf16[8,32,64,128]{3,2,1,0:T(8,128)(2,1)}, u32[]{:S(2)}, u32[]{:S(2)}) async-start(bf16[8,32,64,128]{3,2,1,0:T(8,128)(2,1)} %copy.58), calls=%async_computation | async-start | bytes 8388608 | tf_op jit(solution)/shard_map/all_to_all | solution.py:22
  489.4 66.2 %copy-start.8 = (bf16[32,64,128]{2,1,0:T(8,128)(2,1)S(1)}, bf16[32,64,128]{2,1,0:T(8,128)(2,1)}, u32[]{:S(2)}) copy-start(bf16[32,64,128]{2,1,0:T(8,128)(2,1)} %param.12) | copy-start | bytes 1572868
  545.6 24.7 %all-to-all-start.2 = ((bf16[16,4,64,128]{3,2,1,0:T(8,128)(2,1)}), bf16[16,4,64,128]{3,2,1,0:T(8,128)(2,1)}, u32[]{:S(2)}, u32[]{:S(2)}) async-start(bf16[16,4,64,128]{3,2,1,0:T(8,128)(2,1)} %bitcast_multiply_fusion), calls=%async_computation.3 | async-start | bytes 2097152 | tf_op jit(solution)/shard_map/all_to_all | solution.py:146
  553.0 166.8 %all-reduce.4.cloned.1.call-start = ((), (), s32[]{:S(2)}) async-start(), calls=%async_computation.6 | async-start | bytes 794624 | tf_op jit(solution)/shard_map/psum | solution.py:28
  556.8 0.8 copy-start.10
  574.4 2.2 copy-start.11
  574.5 4.2 copy-start.9
  574.9 4.2 copy-start.4
  574.9 4.2 copy-start.15
Sparse Core Ops, SparseCore 0:
  12.9 92.7 all-gather.1
  111.8 163.4 all-reduce.5
  353.2 102.6 reduce-scatter.1
  581.0 138.6 all-reduce.3
where the time goes:
time: 733 us; the launch traced here: 731 us
  waiting for transfers between devices  533 us (73%)
  local copies, waits for them, and re-layouts  60.6 us (8%)
  matrix products  54.7 us (7%)
  other arithmetic  50.7 us (7%)
  starting transfers between devices  17.1 us (2%)
  between operations  14.8 us (2%)
    psum x1, waiting for transfers between devices, broadcast(): return lax.psum(block, axis)  141 us
    psum x1, waiting for transfers between devices, together(): total = lax.psum(flat, axis)  137 us
    reduce_scatter x1, waiting for transfers between devices, per_device(): lax.psum_scatter(col_partial.astype(jnp.bfloat16), 'row', scatter_dimensi...  103 us
    all_gather x1, waiting for transfers between devices, per_device(): row_panel = lax.all_gather(normed, 'col', axis=1, tiled=True)  92.9 us
    all_to_all x1, waiting for transfers between devices, summed_on_arrival(): tiles = lax.all_to_all(split_up(x, dim, peers), axis, 0, 0, tiled=True)  53 us
    dot_general x4, matrix products, gating(): jnp.einsum('ikc,ch->ikh', panel, weight, preferred_element_type=jnp.float32)  27.1 us
    convert_element_type x2, other arithmetic, gating(): (pad_mask * sigmoid_val * values).astype(jnp.bfloat16)  20.6 us
    convert_element_type x2, local copies, waits for them, and re-layouts, gating(): (pad_mask * sigmoid_val * values).astype(jnp.bfloat16)  20.5 us
  transfers between devices with their start and end apart: 7, of which 6 were waited for; matrix products, arithmetic and copies ran while one was open for 8% of the time, Pallas kernels for 0%

commit v1 on v0

--- a/solution.py
+++ b/solution.py
@@ -25,7 +25,7 @@
 
 def together(arrays, axis):
     flat, at, done = (jnp.concatenate([a.reshape(-1) for a in arrays]), 0, [])
-    total = lax.psum(flat, axis)
+    total = jnp.sum(lax.all_gather(flat, axis), axis=0)
     for a in arrays:
         done.append(total[at : at + a.size].reshape(a.shape))
         at += a.size

time: 733 us -> 991 us (1.35)
  waiting for transfers between devices: 533 us -> 751 us
  other arithmetic: 50.7 us -> 90.8 us
    all_gather x0 -> x1, waiting for transfers between devices: none -> 355 us  [together(): total = jnp.sum(lax.all_gather(flat, axis), axis=0)]
    psum x1 -> x0, waiting for transfers between devices: 137 us -> none  [together(): total = lax.psum(flat, axis)]
    reduce_sum x0 -> x1, other arithmetic: none -> 42.1 us  [together(): total = jnp.sum(lax.all_gather(flat, axis), axis=0)]
  transfers between devices with their start and end apart: 7 -> 7, of which waited for: 6 -> 6; matrix products, arithmetic and copies ran while one was open for 8% -> 6% of each run, Pallas kernels for 0% -> 0%
where the time goes in v1:
time: 991 us; the launch traced here: 989 us
  waiting for transfers between devices  751 us (76%)
  other arithmetic  90.8 us (9%)
  local copies, waits for them, and re-layouts  61 us (6%)
  matrix products  54.4 us (5%)
  starting transfers between devices  17.1 us (2%)
  between operations  14.8 us (1%)
    all_gather x1, waiting for transfers between devices, together(): total = jnp.sum(lax.all_gather(flat, axis), axis=0)  355 us
    psum x1, waiting for transfers between devices, broadcast(): return lax.psum(block, axis)  140 us
    reduce_scatter x1, waiting for transfers between devices, per_device(): lax.psum_scatter(col_partial.astype(jnp.bfloat16), 'row', scatter_dimensi...  103 us
    all_gather x1, waiting for transfers between devices, per_device(): row_panel = lax.all_gather(normed, 'col', axis=1, tiled=True)  92.9 us
    all_to_all x1, waiting for transfers between devices, summed_on_arrival(): tiles = lax.all_to_all(split_up(x, dim, peers), axis, 0, 0, tiled=True)  53 us
    reduce_sum x1, other arithmetic, together(): total = jnp.sum(lax.all_gather(flat, axis), axis=0)  42.1 us
    dot_general x4, matrix products, gating(): jnp.einsum('ikc,ch->ikh', panel, weight, preferred_element_type=jnp.float32)  27.1 us
    convert_element_type x2, other arithmetic, gating(): (pad_mask * sigmoid_val * values).astype(jnp.bfloat16)  20.6 us
  transfers between devices with their start and end apart: 7, of which 6 were waited for; matrix products, arithmetic and copies ran while one was open for 6% of the time, Pallas kernels for 0%

profile of v1, /device:TPU:1, one launch (start us, length us, event | category | flops | bytes accessed | tf_op | source)
XLA Modules:
  0.0 989.0 jit_solution(5004020541183002622)
XLA Ops:
  7.2 1.4 convert_reduce_fusion.1
  8.6 1.7 fusion.33
  10.3 2.5 fusion.27
  12.9 92.9 %all-gather.5.cloned.1.call-done = bf16[32,512,128]{2,1,0:T(8,128)(2,1)} async-done(((bf16[32,64,128]{2,1,0:T(8,128)(2,1)}), bf16[32,512,128]{2,1,0:T(8,128)(2,1)}) %all-gather.5.cloned.1.call-update) | async-done | bytes 4194320 | tf_op jit(solution)/shard_map/all_gather | solution.py:96
  105.7 5.9 broadcast_select_fusion.1
  111.8 0.9 copy-done.5
  112.7 0.4 fusion.19
  113.2 1.4 fusion.78
  114.5 3.1 copy.55
  118.3 0.1 and_convert_fusion.1
  118.4 0.1 and_convert_fusion
  118.5 4.5 fusion.57
  123.0 4.4 fusion.5
  127.4 8.0 copy.53
  135.4 139.9 %all-reduce.3.cloned.1.call-done = (bf16[32,512,128]{2,1,0:T(8,128)(2,1)}, bf16[32,512,128]{2,1,0:T(8,128)(2,1)}) async-done(((bf16[32,512,128]{2,1,0:T(8,128)(2,1)}, bf16[32,512,128]{2,1,0:T(8,128)(2,1)}), (bf16[32,512,128]{2,1,0:T(8,128)(2,1)}, bf16[32,512,128]{2,1,0:T(8,128)(2,1)})) %all-reduce.3.cloned.1.call-update) | async-done | bytes 8388624 | tf_op jit(solution)/shard_map/psum | solution.py:11
  275.3 19.0 %fusion.10 = f32[64,512,256]{2,1,0:T(8,128)} fusion(bf16[32,512,128]{2,1,0:T(8,128)(2,1)} %get-tuple-element.14, bf16[32,512,128]{2,1,0:T(8,128)(2,1)} %get-tuple-element.15, bf16[128,256]{1,0:T(8,128)(2,1)S(1)} %copy-done), kind=kOutput, calls=%fused_computation.14 | convolution fusion | flops 2151677952 | bytes 42008576 | tf_op jit(solution)/shard_map/ikc,ch->ikh/dot_general | solution.py:42
  294.3 16.2 %fusion = bf16[64,512,128]{2,1,0:T(8,128)(2,1)} fusion(f32[64,512,256]{2,1,0:T(8,128)} %fusion.10, f32[64,512]{1,0:T(8,128)S(1)} %and_convert_fusion), kind=kLoop, calls=%fused_computation.1 | loop fusion | flops 25165824 | bytes 42074112 | tf_op jit(solution)/shard_map/convert_element_type | solution.py:46
  310.6 12.5 %copy.52 = bf16[64,512,128]{1,0,2:T(8,128)(2,1)} copy(bf16[64,512,128]{2,1,0:T(8,128)(2,1)} %fusion) | data formatting | bytes 16777216 | tf_op jit(solution)/shard_map/convert_element_type | solution.py:46
  323.1 6.9 bitcast_reduce_fusion
  330.0 0.3 multiply_reduce_fusion.2
  330.4 1.3 multiply_reduce_fusion
  331.7 1.9 multiply_convert_fusion
  333.5 1.0 copy-done.2
  334.5 5.6 convert_bitcast_fusion
  340.1 13.0 %copy.60 = bf16[64,512,128]{2,1,0:T(8,128)(2,1)} copy(bf16[64,512,128]{1,0,2:T(8,128)(2,1)} %convert_bitcast_fusion) | data formatting | bytes 16777216 | tf_op jit(solution)/shard_map/convert_element_type | solution.py:138
  353.1 102.7 %reduce-scatter.2.cloned.1.call-done = bf16[4,512,128]{2,1,0:T(8,128)(2,1)} async-done(((bf16[64,512,128]{2,1,0:T(8,128)(2,1)}), bf16[4,512,128]{2,1,0:T(8,128)(2,1)}) %reduce-scatter.2.cloned.1.call-update) | async-done | bytes 524304 | tf_op jit(solution)/shard_map/reduce_scatter | solution.py:137
  455.8 2.2 copy.61
  458.1 4.1 all-to-all-start.1
  462.2 6.6 convert_bitcast_fusion.1
  468.8 7.9 copy.57
  476.7 5.5 copy.58
  482.2 5.3 all-to-all-start
  487.5 0.1 mul.280
  487.6 1.8 fusion.60
  489.4 1.7 fusion.55
  491.1 0.1 copy.62
  491.2 1.4 bitcast_multiply_fusion
  492.5 53.0 %all-to-all-done = bf16[8,32,64,128]{3,2,1,0:T(8,128)(2,1)} async-done(((bf16[8,32,64,128]{3,2,1,0:T(8,128)(2,1)}), bf16[8,32,64,128]{3,2,1,0:T(8,128)(2,1)}, u32[]{:S(2)}, u32[]{:S(2)}) %all-to-all-start) | async-done | bytes 4194336 | tf_op jit(solution)/shard_map/all_to_all | solution.py:22
  545.5 7.4 all-to-all-start.2
  552.9 0.3 all-gather.7.cloned.1.call-start
  553.1 0.1 and_convert_fusion.2
  553.2 2.2 copy.54
  555.5 1.2 fusion.36
  556.7 0.8 copy-done.10
  557.5 1.3 fusion.67
  558.7 4.1 convert_reduce_fusion
  562.9 7.3 all-to-all-done.2
  570.2 1.1 constant_dynamic-slice_fusion
  571.3 3.1 fusion.51
  574.5 0.4 convolution_bitcast_fusion.3
  574.8 0.4 convolution_add_fusion.1
  575.3 0.4 convolution_bitcast_fusion.2
  575.7 2.1 fusion.32
  577.9 0.1 copy.67
  578.0 0.3 fusion.15
  578.3 0.3 fusion.14
  578.7 1.0 reshape.254
  579.8 3.0 fusion.31
  582.8 355.0 %all-gather.7.cloned.1.call-done = f32[128,1,98816]{2,1,0:T(1,128)} async-done(((f32[1,1,98816]{2,1,0:T(1,128)}), f32[128,1,98816]{2,1,0:T(1,128)}) %all-gather.7.cloned.1.call-update) | async-done | bytes 50593808 | tf_op jit(solution)/shard_map/all_gather | solution.py:28
  937.8 42.1 %reduce_sum.139 = f32[98816]{0:T(1024)S(1)} reduce(f32[128,1,98816]{2,1,0:T(1,128)} %all-gather.7.cloned.1.call-done, f32[]{:T(128)} %constant.51.clone.1), dimensions={0,1}, to_apply=%region_16.17 | reduce | flops 12549632 | bytes 50989060 | tf_op jit(solution)/shard_map/reduce_sum | solution.py:28
  979.9 0.7 fusion.52
  980.5 0.6 fusion.70
  981.1 0.7 mul.297
  981.8 0.7 mul.299
  (58 shorter events, 0.5 us)
Async XLA Ops:
  7.2 268.1 %copy-start = (bf16[128,256]{1,0:T(8,128)(2,1)S(1)}, bf16[128,256]{1,0:T(8,128)(2,1)}, u32[]{:S(2)}) copy-start(bf16[128,256]{1,0:T(8,128)(2,1)} %param.17) | copy-start | bytes 196612
  7.2 98.6 %all-gather.5.cloned.1.call-start = ((), (), s32[]{:S(2)}) async-start(), calls=%async_computation.4 | async-start | bytes 4718592 | tf_op jit(solution)/shard_map/all_gather | solution.py:96
  12.8 262.4 %all-reduce.3.cloned.1.call-start = ((), (), s32[]{:S(2)}) async-start(), calls=%async_computation.7 | async-start | bytes 16777216 | tf_op jit(solution)/shard_map/psum | solution.py:11
  111.7 1.0 copy-start.5
  111.7 1.0 copy-start.14
  111.7 1.4 copy-start.7
  111.7 1.4 copy-start.13
  111.7 6.7 copy-start.12
  111.7 344.1 %reduce-scatter.2.cloned.1.call-start = ((), (), s32[]{:S(2)}) async-start(), calls=%async_computation.5 | async-start | bytes 8912896 | tf_op jit(solution)/shard_map/reduce_scatter | solution.py:137
  323.1 7.3 copy-start.16
  330.0 1.7 copy-start.17
  331.6 2.9 copy-start.1
  333.5 1.0 copy-start.2
  353.1 109.1 %copy-start.3 = (bf16[32,64,128]{1,0,2:T(8,128)(2,1)S(1)}, bf16[32,64,128]{1,0,2:T(8,128)(2,1)}, u32[]{:S(2)}) copy-start(bf16[32,64,128]{1,0,2:T(8,128)(2,1)} %copy-done.2) | copy-start | bytes 1572868
  458.1 24.1 %all-to-all-start.1 = ((bf16[1,4,512,128]{3,1,0,2:T(4,128)(2,1)}), bf16[1,4,512,128]{3,1,0,2:T(4,128)(2,1)S(1)}, u32[]{:S(2)}, u32[]{:S(2)}) async-start(bf16[1,4,512,128]{3,1,0,2:T(4,128)(2,1)} %copy.61), calls=%async_computation.2 | async-start | bytes 1048576 | tf_op jit(solution)/shard_map/all_to_all | solution.py:141
  482.2 5.4 copy-start.6
  482.2 63.3 %all-to-all-start = ((bf16[8,32,64,128]{3,2,1,0:T(8,128)(2,1)}), bf16[8,32,64,128]{3,2,1,0:T(8,128)(2,1)}, u32[]{:S(2)}, u32[]{:S(2)}) async-start(bf16[8,32,64,128]{3,2,1,0:T(8,128)(2,1)} %copy.58), calls=%async_computation | async-start | bytes 8388608 | tf_op jit(solution)/shard_map/all_to_all | solution.py:22
  489.4 66.1 %copy-start.8 = (bf16[32,64,128]{2,1,0:T(8,128)(2,1)S(1)}, bf16[32,64,128]{2,1,0:T(8,128)(2,1)}, u32[]{:S(2)}) copy-start(bf16[32,64,128]{2,1,0:T(8,128)(2,1)} %param.12) | copy-start | bytes 1572868
  545.5 24.7 %all-to-all-start.2 = ((bf16[16,4,64,128]{3,2,1,0:T(8,128)(2,1)}), bf16[16,4,64,128]{3,2,1,0:T(8,128)(2,1)}, u32[]{:S(2)}, u32[]{:S(2)}) async-start(bf16[16,4,64,128]{3,2,1,0:T(8,128)(2,1)} %bitcast_multiply_fusion), calls=%async_computation.3 | async-start | bytes 2097152 | tf_op jit(solution)/shard_map/all_to_all | solution.py:146
  552.9 384.9 %all-gather.7.cloned.1.call-start = ((), (), s32[]{:S(2)}) async-start(), calls=%async_computation.6 | async-start | bytes 50989056 | tf_op jit(solution)/shard_map/all_gather | solution.py:28
  556.7 0.8 copy-start.10
  571.3 3.5 copy-start.9
  574.4 1.2 copy-start.4
  574.5 1.2 copy-start.15
  575.3 2.7 copy-start.11
Sparse Core Ops, SparseCore 0:
  12.9 92.7 all-gather.4
  111.8 163.3 all-reduce.2
  353.2 102.5 reduce-scatter.1
  579.9 357.8 all-gather.6
